TPU v7x, 32 devices: a whole 2x2x4 slice. The times are simulated.
32 devices in a mesh: grp: 4 (over z), mem: 8 (over y, x, core).
Axes of the slice: x: 2, y: 2, z: 4, core: 2. Of those that a mesh axis runs over, the one named last changes fastest.
Arguments:
- embeddings: bfloat16 [32768, 4096], P(('grp', 'mem')), may hold values from -6 to 6
- local_picks: int32 [4, 64], P('grp', 'mem'), may hold values from 0 to 1023
- second_picks: int32 [4, 16], P('grp'), may hold values from 0 to 63
- final_picks: int32 [16], replicated, may hold values from 0 to 63
Outputs:
- gain_table: float32 [64, 64], P('grp', 'mem')
- final_cover: float32 [32768], P(('grp', 'mem'))
Inputs may be any that keep to these rules, and one draw needn't show every extreme that they name: `local_picks`: entry (g, m * 8 + k) names a row among the 1024 points of device m of group g; repeats may occur. `second_picks`: candidate indices of the group, in greedy order; repeats may occur. `final_picks`: index g * 16 + t names group g's second-round pick t; repeats may occur.
All inputs are finite; a program needn't handle non-finite values.
Results may differ from a plain program's by a relative error of at most 0.0003.
Values may be sent and summed in bfloat16 or wider, within the bound.
A program may use at most 64 MiB of HBM per device.

v0:
```python
import jax
import jax.numpy as jnp
from jax import lax
from jax.sharding import PartitionSpec as P

D = 4096


def per_device(embeddings, local_picks, second_picks, final_picks):
    scaling = float(D) ** (-0.5)
    point_count = embeddings.shape[0]
    local_count = local_picks.shape[1]
    second_list = second_picks[0]
    member = lax.axis_index("mem")
    choose = (local_picks[0][:, None] == lax.iota(jnp.int32, point_count)[None, :]).astype(
        jnp.bfloat16
    )
    own_rows = jnp.dot(choose, embeddings, preferred_element_type=jnp.float32).astype(jnp.bfloat16)

    def similar(other_rows):
        dims = (((1,), (1,)), ((), ()))
        return (
            lax.dot_general(embeddings, other_rows, dims, preferred_element_type=jnp.float32)
            * scaling
        )

    candidates = lax.all_gather(own_rows, "mem", axis=0, tiled=True)
    similar_map = similar(candidates)
    cand_total = candidates.shape[0]
    pick_table = (second_list[:, None] == lax.iota(jnp.int32, cand_total)[None, :]).astype(
        jnp.bfloat16
    )
    winners = jnp.dot(pick_table, candidates, preferred_element_type=jnp.float32).astype(
        jnp.bfloat16
    )
    union_rows = lax.all_gather(winners, "grp", axis=0, tiled=True)
    final_table = (
        final_picks[:, None] == lax.iota(jnp.int32, union_rows.shape[0])[None, :]
    ).astype(jnp.bfloat16)
    final_rows = jnp.dot(final_table, union_rows, preferred_element_type=jnp.float32).astype(
        jnp.bfloat16
    )
    own_block = lax.dynamic_slice_in_dim(similar_map, member * local_count, local_count, 1)
    coverage = jnp.max(own_block, axis=1)
    chosen_cols = jnp.take(similar_map, second_list, axis=1)

    def greedy_step(cover_now, column):
        partial_value = jnp.sum(jnp.maximum(similar_map - cover_now[:, None], 0.0), axis=0)
        return (jnp.maximum(cover_now, column), partial_value)

    _, partials = lax.scan(greedy_step, coverage, chosen_cols.T)
    gain_table = lax.psum_scatter(partials, "mem", scatter_dimension=1, tiled=True) / point_count
    final_cover = jnp.max(similar(final_rows), axis=1)
    return (gain_table, final_cover)


def solution(mesh):
    placed = (P(("grp", "mem"), None), P("grp", "mem"), P("grp", None), P())
    return jax.shard_map(
        per_device,
        mesh=mesh,
        in_specs=placed,
        out_specs=(P("grp", "mem"), P(("grp", "mem"))),
        check_vma=False,
    )
```

profile of v0, /device:TPU:0, one launch (start us, length us, event | category | flops | bytes accessed | tf_op | source)
XLA Modules:
  0.0 75.5 jit_solution(6943562138550951512)
XLA Ops:
  0.6 0.0 copy-start.2
  0.6 1.2 %dynamic-slice.4 = u32[1]{0:T(128)} dynamic-slice(u32[32]{0:T(128)} %constant.50, u32[]{:T(128)S(6)} %add.27), dynamic_slice_sizes={1} | dynamic-slice | bytes 12
  2.5 0.7 compare_and_fusion
  3.2 0.7 fusion.7
  3.9 0.0 copy-start
  3.9 4.8 %convolution_convert_fusion.2 = bf16[8,4096]{1,0:T(8,128)(2,1)S(1)} fusion(bf16[1024,4096]{1,0:T(8,128)(2,1)} %param.6, s32[8]{0:T(128)} %bitcast.25), kind=kOutput, calls=%fused_computation.5 | convolution fusion | flops 67149824 | bytes 8454176 | tf_op jit(solution)/shard_map/dot_general | solution.py:18
  8.7 11.3 %all_gather.6 = bf16[64,4096]{1,0:T(8,128)(2,1)S(1)} all-gather(bf16[8,4096]{1,0:T(8,128)(2,1)S(1)} %convolution_convert_fusion.2), channel_id=1, replica_groups=mesh['grp'=4,'mem'=8] {'mem'}, dimensions={0}, use_global_device_ids=true | all-gather | bytes 589824 | tf_op jit(solution)/shard_map/all_gather | solution.py:27
  20.0 0.0 copy-done.2
  20.0 0.2 convolution_convert_fusion.1
  20.2 0.0 copy-done
  20.3 0.0 copy-start.1
  20.3 2.7 %convolution_multiply_fusion = f32[64,1024]{1,0:T(8,128)S(1)} fusion(bf16[64,4096]{1,0:T(8,128)(2,1)S(1)} %all_gather.6, bf16[1024,4096]{1,0:T(8,128)(2,1)S(1)} %copy-done), kind=kOutput, calls=%fused_computation.6 | convolution fusion | flops 536936448 | bytes 9175040 | tf_op jit(solution)/shard_map/dot_general | solution.py:23
  23.0 0.6 gather_fusion
  23.5 0.1 broadcast_select_fusion
  23.6 0.2 copy.8
  23.8 4.8 %while.12 = (s32[]{:T(128)}, f32[1024]{0:T(1024)S(1)}, f32[16,64]{1,0:T(8,128)S(1)}, f32[16,1024]{1,0:T(8,128)S(1)}, f32[1024,64]{1,0:T(8,128)S(1)}, /*index=5*/s32[]{:T(128)}, s32[]{:T(128)}) while((s32[]{:T(128)}, f32[1024]{0:T(1024)S(1)}, f32[16,64]{1,0:T(8,128)S(1)}, f32[16,1024]{1,0:T(8,128)S(1)}, f32[1024,64]{1,0:T(8,128)S(1)}, ...), condition=%wide.region_3.4_spmd, body=%wide.region_1.0_spmd.sunk | while | flops 197570 | bytes 287581 | solution.py:51
  23.8 0.2 maximum_reduce_fusion.2
  24.1 0.2 maximum_reduce_fusion.2
  24.4 0.2 maximum_reduce_fusion.2
  24.7 0.2 maximum_reduce_fusion.2
  25.0 0.2 maximum_reduce_fusion.2
  25.3 0.2 maximum_reduce_fusion.2
  25.6 0.2 maximum_reduce_fusion.2
  25.9 0.2 maximum_reduce_fusion.2
  26.2 0.2 maximum_reduce_fusion.2
  26.5 0.2 maximum_reduce_fusion.2
  26.8 0.2 maximum_reduce_fusion.2
  27.1 0.2 maximum_reduce_fusion.2
  27.5 0.2 maximum_reduce_fusion.2
  27.8 0.2 maximum_reduce_fusion.2
  28.1 0.2 maximum_reduce_fusion.2
  28.4 0.2 maximum_reduce_fusion.2
  28.7 0.1 copy.9
  28.7 23.6 %all-reduce = f32[16,64]{0,1:T(8,128)S(1)} all-reduce(f32[16,64]{0,1:T(8,128)S(1)} %copy.9), channel_id=2, replica_groups=mesh['grp'=4,'mem'=8] {'mem'}, use_global_device_ids=true, to_apply=%region_4.5.clone | all-reduce | flops 1024 | bytes 8192
  52.3 0.6 dynamic-slice_multiply_fusion
  52.9 16.2 %all_gather.7 = bf16[64,4096]{1,0:T(8,128)(2,1)S(1)} all-gather(bf16[16,4096]{1,0:T(8,128)(2,1)S(1)} %convolution_convert_fusion.1), channel_id=1, replica_groups=mesh['grp'=4,'mem'=8] {'grp'}, dimensions={0}, use_global_device_ids=true | all-gather | bytes 655360 | tf_op jit(solution)/shard_map/all_gather | solution.py:36
  69.1 0.0 copy-done.1
  69.1 6.4 %fusion.2 = f32[1024]{0:T(1024)} fusion(bf16[1024,4096]{1,0:T(8,128)(2,1)} %param.6, bf16[64,4096]{1,0:T(8,128)(2,1)S(1)} %all_gather.7, s32[16]{0:T(128)S(1)} %copy-done.1), kind=kOutput, calls=%fused_computation.9 | convolution fusion | flops 142704640 | bytes 8917056 | tf_op jit(solution)/shard_map/dot_general | solution.py:23
  (51 shorter events, 0.9 us)
Async XLA Ops:
  0.6 19.4 %copy-start.2 = (s32[1,16]{1,0:T(1,128)S(1)}, s32[1,16]{1,0:T(1,128)}, u32[]{:S(2)}) copy-start(s32[1,16]{1,0:T(1,128)} %param.8) | copy-start | bytes 196
  3.9 16.4 %copy-start = (bf16[1024,4096]{1,0:T(8,128)(2,1)S(1)}, bf16[1024,4096]{1,0:T(8,128)(2,1)}, u32[]{:S(2)}) copy-start(bf16[1024,4096]{1,0:T(8,128)(2,1)} %param.6) | copy-start | bytes 25165828
  20.3 48.9 %copy-start.1 = (s32[16]{0:T(128)S(1)}, s32[16]{0:T(128)}, u32[]{:S(2)}) copy-start(s32[16]{0:T(128)} %param.9) | copy-start | bytes 196
where the time goes:
time: 75.8 us; the launch traced here: 75.5 us
  blocking collectives  51.1 us (67%)
  matrix products  14.1 us (19%)
  other arithmetic  5.58 us (7%)
  local copies, waits for them, and re-layouts  2.9 us (4%)
  between operations  1.36 us (2%)
    unnamed x1, blocking collectives  23.6 us
    all_gather x1, blocking collectives, per_device(): union_rows = lax.all_gather(winners, 'grp', axis=0, tiled=True)  16.2 us
    all_gather x1, blocking collectives, per_device(): candidates = lax.all_gather(own_rows, 'mem', axis=0, tiled=True)  11.3 us
    dot_general x2, matrix products, similar(): lax.dot_general(embeddings, other_rows, dims, preferred_element_type=jnp....  9.06 us
    dot_general x1, matrix products, per_device(): jnp.dot(choose, embeddings, preferred_element_type=jnp.float32)  4.78 us
    reduce_sum x16, other arithmetic, greedy_step(): jnp.sum(jnp.maximum(similar_map - cover_now[:, None], 0.0), axis=0)  3.49 us

commit v1 on v0

--- a/solution.py
+++ b/solution.py
@@ -1,9 +1,37 @@
+import functools
 import jax
 import jax.numpy as jnp
 from jax import lax
 from jax.sharding import PartitionSpec as P
 
 D = 4096
+
+
+def _save_series_all(vec, along_dim):
+    vec = jnp.moveaxis(vec, 0, along_dim)
+    far_arr = vec.shape
+    return vec.reshape(
+        *far_arr[:along_dim], far_arr[along_dim] * far_arr[along_dim + 1], *far_arr[along_dim + 2 :]
+    )
+
+
+def cut_the_vector(x_part, bus_axis):
+    degree = lax.axis_size(bus_axis)
+    y1 = x_part[None]
+    for i in range(degree.bit_length() - 1):
+        arr_out = 1 << i
+        oldest = lax.ppermute(y1, bus_axis, [(q, q ^ arr_out) for q in range(degree)])
+        latest = jnp.stack([y1, oldest], axis=0)
+        b_next = lax.axis_index(bus_axis) >> i & 1
+        y1 = jnp.where(b_next == 0, latest, latest[::-1]).reshape(-1, *x_part.shape)
+    return y1
+
+
+def begin_things_on_mesh(here_x, my_tile, dim_no):
+    return _save_series_all(cut_the_vector(here_x, my_tile), dim_no)
+
+
+use_body = functools.partial(begin_things_on_mesh, my_tile="grp", dim_no=0)
 
 
 def per_device(embeddings, local_picks, second_picks, final_picks):
@@ -33,7 +61,7 @@
     winners = jnp.dot(pick_table, candidates, preferred_element_type=jnp.float32).astype(
         jnp.bfloat16
     )
-    union_rows = lax.all_gather(winners, "grp", axis=0, tiled=True)
+    union_rows = use_body(winners)
     final_table = (
         final_picks[:, None] == lax.iota(jnp.int32, union_rows.shape[0])[None, :]
     ).astype(jnp.bfloat16)

time: 75.8 us -> 62 us (0.82)
  blocking collectives: 51.1 us -> 34.3 us
  starting transfers between devices: 0 us -> 4.3 us
  other arithmetic: 5.58 us -> 4.49 us
    all_gather x1 -> x0, blocking collectives: 16.2 us -> none  [per_device(): union_rows = lax.all_gather(winners, 'grp', axis=0, tiled=True)]
    ppermute x0 -> x2, starting transfers between devices: none -> 4.3 us  [cut_the_vector(): lax.ppermute(y1, bus_axis, [(q, q ^ arr_out) for q in range(degree)])]
    unnamed x1, blocking collectives: 23.6 us -> 22.8 us
  transfers between devices with their start and end apart: 0 -> 2, of which waited for: 0 -> 1; matrix products, arithmetic and copies ran while one was open for 0% -> 15% of each run, Pallas kernels for 0% -> 0%
where the time goes in v1:
time: 62 us; the launch traced here: 61.8 us
  blocking collectives  34.3 us (55%)
  matrix products  14.1 us (23%)
  other arithmetic  4.49 us (7%)
  starting transfers between devices  4.3 us (7%)
  local copies, waits for them, and re-layouts  2.23 us (4%)
  between operations  1.44 us (2%)
    unnamed x1, blocking collectives  22.8 us
    all_gather x1, blocking collectives, per_device(): candidates = lax.all_gather(own_rows, 'mem', axis=0, tiled=True)  11.5 us
    dot_general x2, matrix products, similar(): lax.dot_general(embeddings, other_rows, dims, preferred_element_type=jnp....  9.06 us
    dot_general x1, matrix products, per_device(): jnp.dot(choose, embeddings, preferred_element_type=jnp.float32)  4.78 us
    ppermute x2, starting transfers between devices, cut_the_vector(): lax.ppermute(y1, bus_axis, [(q, q ^ arr_out) for q in range(degree)])  4.3 us
    reduce_sum x16, other arithmetic, greedy_step(): jnp.sum(jnp.maximum(similar_map - cover_now[:, None], 0.0), axis=0)  3.48 us
  transfers between devices with their start and end apart: 2, of which 1 were waited for; matrix products, arithmetic and copies ran while one was open for 15% of the time, Pallas kernels for 0%

profile of v1, /device:TPU:0, one launch (start us, length us, event | category | flops | bytes accessed | tf_op | source)
XLA Modules:
  0.0 61.8 jit_solution(470589077535064936)
XLA Ops:
  0.6 0.0 slice-start
  0.6 0.0 copy-start.1
  0.7 0.0 slice-start.1
  0.7 4.8 %convolution_convert_fusion.2 = bf16[8,4096]{1,0:T(8,128)(2,1)S(1)} fusion(bf16[1024,4096]{1,0:T(8,128)(2,1)} %param.6, s32[8]{0:T(128)} %bitcast.41), kind=kOutput, calls=%fused_computation.5 | convolution fusion | flops 67149824 | bytes 8454176 | tf_op jit(solution)/shard_map/dot_general | solution.py:46
  5.4 11.5 %all_gather.3 = bf16[64,4096]{1,0:T(8,128)(2,1)S(1)} all-gather(bf16[8,4096]{1,0:T(8,128)(2,1)S(1)} %convolution_convert_fusion.2), channel_id=1, replica_groups=mesh['grp'=4,'mem'=8] {'mem'}, dimensions={0}, use_global_device_ids=true | all-gather | bytes 589824 | tf_op jit(solution)/shard_map/all_gather | solution.py:55
  16.9 0.0 copy-done.1
  16.9 0.2 convolution_convert_fusion.1
  17.1 1.6 %collective-permute-start = (bf16[1,16,4096]{2,1,0:T(8,128)(2,1)S(1)}, bf16[1,16,4096]{2,1,0:T(8,128)(2,1)S(1)}, u32[]{:S(2)}, u32[]{:S(2)}) collective-permute-start(bf16[1,16,4096]{2,1,0:T(8,128)(2,1)S(1)} %bitcast.35), channel_id=1, source_target_pairs={{0,8},{8,0},{16,24},{24,16},{1,9},{9,1},{17,25},{25,17},{2,10},{10... | collective-permute-start | bytes 393224 | tf_op jit(solution)/shard_map/ppermute | solution.py:23
  18.8 0.0 slice-done
  18.8 0.0 slice-done.1
  18.8 0.0 copy-start.2
  18.8 2.7 %convolution_multiply_fusion = f32[64,1024]{1,0:T(8,128)S(1)} fusion(bf16[64,4096]{1,0:T(8,128)(2,1)S(1)} %all_gather.3, bf16[1024,4096]{1,0:T(8,128)(2,1)S(1)} %bitcast.31), kind=kOutput, calls=%fused_computation.6 | convolution fusion | flops 536936448 | bytes 9175040 | tf_op jit(solution)/shard_map/dot_general | solution.py:51
  21.5 0.0 copy-start
  21.5 0.2 copy.8
  21.8 0.6 gather_fusion
  22.3 0.1 broadcast_select_fusion
  22.4 0.5 collective-permute-done
  23.0 0.1 fusion.4
  23.1 2.7 %collective-permute-start.1 = (bf16[2,16,4096]{2,1,0:T(8,128)(2,1)S(1)}, bf16[2,16,4096]{2,1,0:T(8,128)(2,1)S(1)}, u32[]{:S(2)}, u32[]{:S(2)}) collective-permute-start(bf16[2,16,4096]{2,1,0:T(8,128)(2,1)S(1)} %get-tuple-element.51), channel_id=1, source_target_pairs={{0,16},{8,24},{16,0},{24,8},{1,17},{9,25},{17,1},{25,9},{2,18},{10... | collective-permute-start | bytes 786440 | tf_op jit(solution)/shard_map/ppermute | solution.py:23
  25.7 4.8 %while.12 = (s32[]{:T(128)}, f32[1024]{0:T(1024)S(1)}, f32[16,64]{1,0:T(8,128)S(1)}, f32[16,1024]{1,0:T(8,128)S(1)}, f32[1024,64]{1,0:T(8,128)S(1)}, /*index=5*/s32[]{:T(128)}, s32[]{:T(128)}) while((s32[]{:T(128)}, f32[1024]{0:T(1024)S(1)}, f32[16,64]{1,0:T(8,128)S(1)}, f32[16,1024]{1,0:T(8,128)S(1)}, f32[1024,64]{1,0:T(8,128)S(1)}, ...), condition=%wide.region_3.4_spmd, body=%wide.region_1.3_spmd.sunk | while | flops 197570 | bytes 287573 | solution.py:79
  25.7 0.2 maximum_reduce_fusion.2
  26.0 0.2 maximum_reduce_fusion.2
  26.3 0.2 maximum_reduce_fusion.2
  26.6 0.2 maximum_reduce_fusion.2
  26.9 0.2 maximum_reduce_fusion.2
  27.2 0.2 maximum_reduce_fusion.2
  27.5 0.2 maximum_reduce_fusion.2
  27.8 0.2 maximum_reduce_fusion.2
  28.1 0.2 maximum_reduce_fusion.2
  28.4 0.2 maximum_reduce_fusion.2
  28.7 0.2 maximum_reduce_fusion.2
  29.0 0.2 maximum_reduce_fusion.2
  29.3 0.2 maximum_reduce_fusion.2
  29.6 0.2 maximum_reduce_fusion.2
  29.9 0.2 maximum_reduce_fusion.2
  30.2 0.2 maximum_reduce_fusion.2
  30.5 0.1 copy.9
  30.6 0.0 copy-done.2
  30.6 0.6 dynamic-slice.4
  31.9 22.8 %all-reduce = f32[16,64]{0,1:T(8,128)S(1)} all-reduce(f32[16,64]{0,1:T(8,128)S(1)} %copy.9), channel_id=2, replica_groups=mesh['grp'=4,'mem'=8] {'mem'}, use_global_device_ids=true, to_apply=%region_4.5.clone | all-reduce | flops 1024 | bytes 8192
  54.7 0.6 dynamic-slice_multiply_fusion
  55.3 0.0 collective-permute-done.1
  55.3 0.1 pad_maximum_fusion
  55.3 0.1 reverse_select_fusion
  55.4 0.0 copy-done
  55.4 6.4 %fusion.2 = f32[1024]{0:T(1024)} fusion(bf16[1024,4096]{1,0:T(8,128)(2,1)} %param.6, bf16[64,4096]{1,0:T(8,128)(2,1)S(1)} %bitcast.34, s32[16]{0:T(128)S(1)} %copy-done), kind=kOutput, calls=%fused_computation.9 | convolution fusion | flops 142704640 | bytes 8917056 | tf_op jit(solution)/shard_map/dot_general | solution.py:51
  (55 shorter events, 0.9 us)
Async XLA Ops:
  0.6 18.2 %slice-start = ((s8[8388608]{0:T(1024)(128)(4,1)}), s8[4194304]{0:T(1024)(128)(4,1)S(1)}, s32[]{:S(2)}) async-start(s8[8388608]{0:T(1024)(128)(4,1)} %bitcast.30), calls=%async_computation | async-start | bytes 8388608
  0.6 16.3 %copy-start.1 = (s32[1,16]{1,0:T(1,128)S(1)}, s32[1,16]{1,0:T(1,128)}, u32[]{:S(2)}) copy-start(s32[1,16]{1,0:T(1,128)} %param.8) | copy-start | bytes 196
  0.7 18.1 %slice-start.1 = ((s8[8388608]{0:T(1024)(128)(4,1)}), s8[4194304]{0:T(1024)(128)(4,1)S(1)}, s32[]{:S(2)}) async-start(s8[8388608]{0:T(1024)(128)(4,1)} %bitcast.30), calls=%async_computation.1 | async-start | bytes 8388608
  17.1 5.8 %collective-permute-start = (bf16[1,16,4096]{2,1,0:T(8,128)(2,1)S(1)}, bf16[1,16,4096]{2,1,0:T(8,128)(2,1)S(1)}, u32[]{:S(2)}, u32[]{:S(2)}) collective-permute-start(bf16[1,16,4096]{2,1,0:T(8,128)(2,1)S(1)} %bitcast.35), channel_id=1, source_target_pairs={{0,8},{8,0},{16,24},{24,16},{1,9},{9,1},{17,25},{25,17},{2,10},{10... | collective-permute-start | bytes 393224 | tf_op jit(solution)/shard_map/ppermute | solution.py:23
  18.8 11.8 %copy-start.2 = (u32[32]{0:T(128)S(1)}, u32[32]{0:T(128)}, u32[]{:S(2)}) copy-start(u32[32]{0:T(128)} %constant.56) | copy-start | bytes 388
  21.5 34.0 %copy-start = (s32[16]{0:T(128)S(1)}, s32[16]{0:T(128)}, u32[]{:S(2)}) copy-start(s32[16]{0:T(128)} %param.9) | copy-start | bytes 196
  23.1 32.2 %collective-permute-start.1 = (bf16[2,16,4096]{2,1,0:T(8,128)(2,1)S(1)}, bf16[2,16,4096]{2,1,0:T(8,128)(2,1)S(1)}, u32[]{:S(2)}, u32[]{:S(2)}) collective-permute-start(bf16[2,16,4096]{2,1,0:T(8,128)(2,1)S(1)} %get-tuple-element.51), channel_id=1, source_target_pairs={{0,16},{8,24},{16,0},{24,8},{1,17},{9,25},{17,1},{25,9},{2,18},{10... | collective-permute-start | bytes 786440 | tf_op jit(solution)/shard_map/ppermute | solution.py:23
